TPU v7x, 32 devices: a whole 2x2x4 slice. The times are simulated.
32 devices in a mesh: eq: 2 (over x), row: 4 (over y, core), col: 4 (over z).
Axes of the slice: x: 2, y: 2, z: 4, core: 2. Of those that a mesh axis runs over, the one named last changes fastest.
Arguments:
- transition: float32 [6144, 3072], P(('eq', 'row'), 'col'), parts along dimension 0, may hold values from -0.05 to 0.9
- covariance: float32 [6144, 3072], P(('eq', 'row'), 'col'), parts along dimension 0, may hold values from -1 to 5, as said below
Outputs:
- covariance_out: float32 [6144, 3072], P(('eq', 'row'), 'col'), parts along dimension 0
- transition_out: float32 [6144, 3072], P(('eq', 'row'), 'col'), parts along dimension 0
There are 2 independent parts, one for each index of `eq`. A program takes and returns all parts, laid end to end along the dimension named above; each array names one. Nothing has to cross between parts.
Inputs may be any that keep to these rules, and one draw needn't show every extreme that they name: covariance is exactly symmetric.
All inputs are finite; a program needn't handle non-finite values.
Results may differ from a plain program's by a relative error of at most 0.0001.
Values sent between devices are 32-bit elements; how exact they have to be, the bound alone decides.
A program may use at most 128 MiB of HBM per device.

v0:
```python
import jax
import jax.numpy as jnp
from jax import lax
from jax.sharding import PartitionSpec as P


def per_device(transition, covariance):
    highest = lax.Precision.HIGHEST
    current = covariance
    matrix_row = lax.all_gather(transition, "col", axis=1, tiled=True)

    def add_one(pieces):
        return jnp.dot(matrix_row, pieces, precision=highest, preferred_element_type=jnp.float32)

    row_slices = lax.all_to_all(
        lax.all_to_all(transition, "row", split_axis=0, concat_axis=1, tiled=True),
        "col",
        split_axis=1,
        concat_axis=1,
        tiled=True,
    )
    product = add_one(lax.all_gather(current, "row", axis=0, tiled=True))
    squared = add_one(lax.all_gather(transition, "row", axis=0, tiled=True))
    product_row = lax.all_gather(product, "col", axis=1, tiled=True)
    update = lax.dot_general(
        product_row,
        lax.all_gather(row_slices, "row", axis=0, tiled=True),
        (((1,), (1,)), ((), ())),
        precision=highest,
        preferred_element_type=jnp.float32,
    )
    current = update + current
    return (current, squared)


def solution(mesh):
    return jax.shard_map(
        per_device,
        mesh=mesh,
        in_specs=(P(("eq", "row"), "col"), P(("eq", "row"), "col")),
        out_specs=(P(("eq", "row"), "col"), P(("eq", "row"), "col")),
        check_vma=False,
    )
```

profile of v0, /device:TPU:0, one launch (start us, length us, event | category | flops | bytes accessed | tf_op | source)
XLA Modules:
  0.0 605.5 jit_solution(9923091636029613894)
XLA Ops:
  7.2 0.0 all-gather.8.cloned.1.call-start
  7.2 0.7 all-gather.8.cloned.1.call-update
  7.9 0.0 all-gather.6.cloned.1.call-start
  7.9 0.7 all-gather.6.cloned.1.call-update
  8.6 0.0 all-gather.14.cloned.1.call-start
  8.7 0.7 all-gather.14.cloned.1.call-update
  9.4 0.0 all-gather.12.cloned.1.call-start
  9.4 51.7 %all_to_all.25 = f32[4,192,768]{2,1,0:T(8,128)S(1)} all-to-all(f32[4,192,768]{2,1,0:T(8,128)} %bitcast.10), channel_id=1, replica_groups=mesh['eq'=2,'row'=4,'col'=4] {'row'}, dimensions={0} | all-to-all | bytes 4718592 | tf_op jit(solution)/shard_map/all_to_all | solution.py:16
  61.1 88.7 %all_to_all.26 = f32[192,4,768]{2,0,1:T(8,128)S(1)} all-to-all(f32[192,4,768]{2,0,1:T(8,128)S(1)} %bitcast.13), channel_id=1, replica_groups=mesh['eq'=2,'row'=4,'col'=4] {'col'}, dimensions={1} | all-to-all | bytes 4718592 | tf_op jit(solution)/shard_map/all_to_all | solution.py:15
  149.8 1.6 copy.6
  151.5 0.0 all-gather.12.cloned.1.call-update
  151.5 0.0 all-gather.10.cloned.1.call-start
  151.5 0.0 all-gather.8.cloned.1.call-done
  151.6 121.3 %all-gather.6.cloned.1.call-done = f32[768,3072]{1,0:T(8,128)} async-done(((f32[768,768]{1,0:T(8,128)}), f32[768,3072]{1,0:T(8,128)}) %all-gather.6.cloned.1.call-update) | async-done | bytes 9437200 | tf_op jit(solution)/shard_map/all_gather | solution.py:10
  272.8 27.4 %fusion = f32[768,768]{1,0:T(8,128)} fusion(f32[768,3072]{1,0:T(8,128)} %all-gather.6.cloned.1.call-done, f32[3072,768]{1,0:T(8,128)} %all-gather.8.cloned.1.call-done), kind=kOutput, calls=%fused_computation.1 | convolution fusion | flops 21743271936 | bytes 21233664 | tf_op jit(solution)/shard_map/dot_general | solution.py:13
  300.2 0.0 all-gather.10.cloned.1.call-update
  300.3 0.0 copy-start
  300.3 36.6 %all-gather.14.cloned.1.call-done = f32[3072,768]{1,0:T(8,128)} async-done(((f32[768,768]{1,0:T(8,128)}), f32[3072,768]{1,0:T(8,128)}) %all-gather.14.cloned.1.call-update) | async-done | bytes 9437200 | tf_op jit(solution)/shard_map/all_gather | solution.py:23
  336.9 27.4 %fusion.1 = f32[768,768]{1,0:T(8,128)} fusion(f32[768,3072]{1,0:T(8,128)} %all-gather.6.cloned.1.call-done, f32[3072,768]{1,0:T(8,128)} %all-gather.14.cloned.1.call-done), kind=kOutput, calls=%fused_computation.2 | convolution fusion | flops 21743271936 | bytes 21233664 | tf_op jit(solution)/shard_map/dot_general | solution.py:13
  364.3 38.3 %all-gather.12.cloned.1.call-done = f32[768,3072]{1,0:T(8,128)} async-done(((f32[192,3072]{1,0:T(8,128)}), f32[768,3072]{1,0:T(8,128)}) %all-gather.12.cloned.1.call-update) | async-done | bytes 9437200 | tf_op jit(solution)/shard_map/all_gather | solution.py:27
  402.5 168.8 %all-gather.10.cloned.1.call-done = f32[768,3072]{1,0:T(8,128)} async-done(((f32[768,768]{1,0:T(8,128)}), f32[768,3072]{1,0:T(8,128)}) %all-gather.10.cloned.1.call-update) | async-done | bytes 9437200 | tf_op jit(solution)/shard_map/all_gather | solution.py:24
  571.3 0.0 copy-done
  571.3 27.7 %convolution_add_fusion = f32[768,768]{1,0:T(8,128)} fusion(f32[768,768]{1,0:T(8,128)S(1)} %copy-done, f32[768,3072]{1,0:T(8,128)} %all-gather.10.cloned.1.call-done, f32[768,3072]{1,0:T(8,128)} %all-gather.12.cloned.1.call-done), kind=kOutput, calls=%fused_computation | convolution fusion | flops 21743861760 | bytes 23592960 | tf_op jit(solution)/shard_map/dot_general | solution.py:25
Async XLA Ops:
  7.2 144.4 %all-gather.8.cloned.1.call-start = ((), (), s32[]{:S(2)}) async-start(), calls=%async_computation.3 | async-start | bytes 11796480 | tf_op jit(solution)/shard_map/all_gather | solution.py:22
  7.9 264.9 %all-gather.6.cloned.1.call-start = ((), (), s32[]{:S(2)}) async-start(), calls=%async_computation.2 | async-start | bytes 11796480 | tf_op jit(solution)/shard_map/all_gather | solution.py:10
  8.6 328.2 %all-gather.14.cloned.1.call-start = ((), (), s32[]{:S(2)}) async-start(), calls=%async_computation.6 | async-start | bytes 11796480 | tf_op jit(solution)/shard_map/all_gather | solution.py:23
  9.4 393.2 %all-gather.12.cloned.1.call-start = ((), (), s32[]{:S(2)}) async-start(), calls=%async_computation.5 | async-start | bytes 11796480 | tf_op jit(solution)/shard_map/all_gather | solution.py:27
  151.5 419.8 %all-gather.10.cloned.1.call-start = ((), (), s32[]{:S(2)}) async-start(), calls=%async_computation.4 | async-start | bytes 11796480 | tf_op jit(solution)/shard_map/all_gather | solution.py:24
  300.3 271.0 %copy-start = (f32[768,768]{1,0:T(8,128)S(1)}, f32[768,768]{1,0:T(8,128)}, u32[]{:S(2)}) copy-start(f32[768,768]{1,0:T(8,128)} %param.3) | copy-start | bytes 7077892
Sparse Core Ops, SparseCore 0:
  9.5 85.0 all-gather.7
  96.2 176.6 all-gather.5
  274.4 62.4 all-gather.13
  338.3 64.2 all-gather.11
  404.5 166.7 all-gather.9
where the time goes:
time: 606 us
  waiting for transfers between devices  367 us (61%)
  blocking collectives  140 us (23%)
  matrix products  82.5 us (14%)
  between operations  13.8 us (2%)
    all_gather x1, waiting for transfers between devices, per_device(): product_row = lax.all_gather(product, 'col', axis=1, tiled=True)  169 us
    all_gather x1, waiting for transfers between devices, per_device(): matrix_row = lax.all_gather(transition, 'col', axis=1, tiled=True)  121 us
    all_to_all x1, blocking collectives, per_device(): lax.all_to_all(lax.all_to_all(transition, 'row', split_axis=0, concat_axi...  88.7 us
    dot_general x2, matrix products, add_one(): jnp.dot(matrix_row, pieces, precision=highest, preferred_element_type=jnp...  54.8 us
    all_to_all x1, blocking collectives, per_device(): lax.all_to_all(transition, 'row', split_axis=0, concat_axis=1, tiled=True)  51.7 us
    all_gather x1, waiting for transfers between devices, per_device(): lax.all_gather(row_slices, 'row', axis=0, tiled=True)  38.3 us
    all_gather x1, waiting for transfers between devices, per_device(): squared = add_one(lax.all_gather(transition, 'row', axis=0, tiled=True))  36.6 us
    dot_general x1, matrix products, per_device(): lax.dot_general(product_row, lax.all_gather(row_slices, 'row', axis=0, ti...  27.7 us
  transfers between devices with their start and end apart: 5, of which 4 were waited for; matrix products, arithmetic and copies ran while one was open for 9% of the time, Pallas kernels for 0%

commit v1 on v0

v1 whole, which is shorter than its diff:
```python
import functools

import jax
import jax.numpy as jnp
from jax import lax
from jax.experimental import pallas as pl
from jax.experimental.pallas import tpu as pltpu
from jax.sharding import PartitionSpec as P

CHUNKS = 4
TILE = 256
LEFT, RIGHT = 0, 1


def split(value):
    high = value.astype(jnp.bfloat16)
    return high, (value - high.astype(jnp.float32)).astype(jnp.bfloat16)


def product(left, right, transposed=False):
    dims = (((1,), (1 if transposed else 0,)), ((), ()))
    dot = functools.partial(lax.dot_general, dimension_numbers=dims, preferred_element_type=jnp.float32)
    return dot(left[0], right[0]) + (dot(left[0], right[1]) + dot(left[1], right[0]))


def kernel(
    n, a_ref, x_ref, update_ref, square_ref,
    a_row, a_col, x_col, partial, arrived, y_high, y_low,
    local_sems, row_send, row_recv, gather_send, gather_recv, reduce_send, reduce_recv,
):
    r, z = lax.axis_index("row"), lax.axis_index("col")
    size = a_ref.shape[0]
    step = size // CHUNKS
    far = lax.rem(r + n // 2, n)
    near = r + 1 - 2 * lax.rem(r, 2)

    def block_of(m):
        base = jnp.where(lax.rem(m, 2) == 0, r, near)
        return lax.rem(base + (m // 2) * 2, n)

    def rows(c):
        return pl.ds(c * step, step)

    local = [
        pltpu.make_async_copy(a_ref, a_row.at[z], local_sems.at[0]),
        pltpu.make_async_copy(a_ref, a_col.at[r], local_sems.at[1]),
        pltpu.make_async_copy(x_ref, x_col.at[r], local_sems.at[2]),
    ]
    for copy in local:
        copy.start()

    barrier = pltpu.get_barrier_semaphore()
    pl.semaphore_signal(barrier, inc=1, device_id={"row": far}, device_id_type=pl.DeviceIdType.MESH)
    pl.semaphore_signal(barrier, inc=1, device_id={"row": near}, device_id_type=pl.DeviceIdType.MESH)

    @pl.when(z > 0)
    def _():
        pl.semaphore_signal(barrier, inc=1, device_id={"col": z - 1}, device_id_type=pl.DeviceIdType.MESH)

    @pl.when(z < n - 1)
    def _():
        pl.semaphore_signal(barrier, inc=1, device_id={"col": z + 1}, device_id_type=pl.DeviceIdType.MESH)

    pl.semaphore_wait(barrier, 4 - jnp.where(z == 0, 1, 0) - jnp.where(z == n - 1, 1, 0))

    for copy in local:
        copy.wait()

    def row_copy(which, kind):
        buffer = (x_col, a_col)[which]
        block = far if kind == 2 else r
        return pltpu.make_async_remote_copy(
            src_ref=buffer.at[block],
            dst_ref=buffer.at[block],
            send_sem=row_send.at[which, kind],
            recv_sem=row_recv.at[which, kind],
            device_id={"row": far if kind == 0 else near},
            device_id_type=pl.DeviceIdType.MESH,
        )

    def row_wait(which, kind):
        buffer = (x_col, a_col)[which]
        block = (far, near, lax.rem(near + n // 2, n))[kind]
        pltpu.make_async_remote_copy(
            src_ref=buffer.at[block],
            dst_ref=buffer.at[block],
            send_sem=row_send.at[which, kind],
            recv_sem=row_recv.at[which, kind],
            device_id={"row": near},
            device_id_type=pl.DeviceIdType.MESH,
        ).wait_recv()

    def gather_copy(side, hop, c, block, target):
        return pltpu.make_async_remote_copy(
            src_ref=a_row.at[block, rows(c)],
            dst_ref=a_row.at[block, rows(c)],
            send_sem=gather_send.at[side, hop, c],
            recv_sem=gather_recv.at[side, hop, c],
            device_id={"col": target},
            device_id_type=pl.DeviceIdType.MESH,
        )

    def gather_each(hop, c, act):
        @pl.when((z > 0) & (z + hop <= n - 1))
        def _():
            act(gather_copy(LEFT, hop, c, z + hop, z - 1))

        @pl.when((z < n - 1) & (z - hop >= 0))
        def _():
            act(gather_copy(RIGHT, hop, c, z - hop, z + 1))

    def gather_send_hop(hop, c):
        gather_each(hop, c, lambda copy: copy.start())

    def gather_wait(hop, c):
        @pl.when(z + 1 + hop <= n - 1)
        def _():
            gather_copy(LEFT, hop, c, z + 1 + hop, z + 1).wait_recv()

        @pl.when(z - 1 - hop >= 0)
        def _():
            gather_copy(RIGHT, hop, c, z - 1 - hop, z - 1).wait_recv()

    def forward(hop, c):
        gather_wait(hop, c)
        gather_send_hop(hop + 1, c)

    def multiply(c, column, store):
        def tile(t, carry):
            lanes = pl.ds(pl.multiple_of(t * TILE, TILE), TILE)

            def one(k, total):
                return total + product(split(a_row[k, rows(c)]), split(column[k, :, lanes]))

            store(lanes, lax.fori_loop(0, n, one, jnp.zeros((step, TILE), jnp.float32)))
            return carry

        lax.fori_loop(0, size // TILE, tile, 0)

    def compute_y(c):
        def store(lanes, value):
            high, low = split(value)
            y_high[rows(c), lanes] = high
            y_low[rows(c), lanes] = low

        multiply(c, x_col, store)

    def compute_square(c):
        def store(lanes, value):
            square_ref[rows(c), lanes] = value

        multiply(c, a_col, store)

    def reduce_copy(side, d, m, c):
        slot = d if side == LEFT else jnp.where(d == z + 1, n, d)
        return pltpu.make_async_remote_copy(
            src_ref=partial.at[d, rows(c)],
            dst_ref=arrived.at[slot, rows(c)],
            send_sem=reduce_send.at[m, c],
            recv_sem=reduce_recv.at[slot, c],
            device_id={"col": z - 1 if side == LEFT else z + 1},
            device_id_type=pl.DeviceIdType.MESH,
        )

    def reduce_wait(slot, c):
        pltpu.make_async_remote_copy(
            src_ref=arrived.at[slot, rows(c)],
            dst_ref=arrived.at[slot, rows(c)],
            send_sem=reduce_send.at[0, c],
            recv_sem=reduce_recv.at[slot, c],
            device_id={"row": near},
            device_id_type=pl.DeviceIdType.MESH,
        ).wait_recv()

    def start_partials(c, low, high):
        per = size // TILE

        def tile(i, carry):
            d = block_of(i // per)
            lanes = pl.ds(pl.multiple_of(lax.rem(i, per) * TILE, TILE), TILE)
            partial[d, rows(c), lanes] = product(
                (y_high[rows(c)], y_low[rows(c)]), split(a_col[d, lanes]), transposed=True
            )
            return carry

        lax.fori_loop(low * per, high * per, tile, 0)

        def send(m, carry):
            d = block_of(m)

            @pl.when((z == n - 1) & (d < z))
            def _():
                reduce_copy(LEFT, d, m, c).start()

            @pl.when((z == 0) & (d > z))
            def _():
                reduce_copy(RIGHT, d, m, c).start()

            return carry

        lax.fori_loop(low, high, send, 0)

    def pass_on(hop, c, low, high):
        def one(m, carry):
            d = block_of(m)

            def add():
                reduce_wait(d, c)
                partial[d, rows(c)] = partial[d, rows(c)] + arrived[d, rows(c)]

            @pl.when((z == n - 1 - hop) & (d < z))
            def _():
                add()
                reduce_copy(LEFT, d, m, c).start()

            @pl.when((z == hop) & (d > z))
            def _():
                add()
                reduce_copy(RIGHT, d, m, c).start()

            return carry

        lax.fori_loop(low, high, one, 0)

    def finish(c):
        update_ref[rows(c)] = x_col[r, rows(c)] + partial[z, rows(c)]

        @pl.when(z < n - 1)
        def _():
            reduce_wait(z, c)
            update_ref[rows(c)] = update_ref[rows(c)] + arrived[z, rows(c)]

        @pl.when(z > 0)
        def _():
            reduce_wait(n, c)
            update_ref[rows(c)] = update_ref[rows(c)] + arrived[n, rows(c)]

    half = n // 2
    gather_send_hop(0, 0)
    for which in range(2):
        row_copy(which, 0).start()
        row_copy(which, 1).start()
    forward(0, 0)
    forward(1, 0)
    gather_send_hop(0, 1)
    forward(0, 1)
    row_wait(0, 0)
    row_copy(0, 2).start()
    forward(1, 1)
    gather_send_hop(0, 2)
    row_wait(0, 1)
    row_wait(0, 2)
    row_wait(1, 1)
    gather_wait(2, 0)
    compute_y(0)
    start_partials(0, 0, half)
    forward(0, 2)
    pass_on(1, 0, 0, half)
    forward(1, 2)
    gather_send_hop(0, 3)
    gather_wait(2, 1)
    compute_y(1)
    start_partials(1, 0, half)
    pass_on(2, 0, 0, half)
    row_wait(1, 0)
    row_copy(1, 2).start()
    pass_on(1, 1, 0, half)
    row_wait(1, 2)
    start_partials(0, half, n)
    start_partials(1, half, n)
    forward(0, 3)
    pass_on(2, 1, 0, half)
    pass_on(1, 0, half, n)
    forward(1, 3)
    pass_on(1, 1, half, n)
    gather_wait(2, 2)
    compute_y(2)
    start_partials(2, 0, n)
    pass_on(2, 0, half, n)
    pass_on(2, 1, half, n)
    compute_square(0)
    pass_on(1, 2, 0, n)
    gather_wait(2, 3)
    compute_y(3)
    start_partials(3, 0, n)
    pass_on(2, 2, 0, n)
    compute_square(1)
    pass_on(1, 3, 0, n)
    compute_square(2)
    pass_on(2, 3, 0, n)
    compute_square(3)
    for c in range(CHUNKS):
        finish(c)

    for which in range(2):
        for kind in range(3):
            row_copy(which, kind).wait_send()
    for c in range(CHUNKS):
        for hop in range(n - 1):
            gather_each(hop, c, lambda copy: copy.wait_send())

        def wait_sent(m, carry):
            d = block_of(m)

            @pl.when(d != z)
            def _():
                reduce_copy(LEFT, d, m, c).wait_send()

            return carry

        lax.fori_loop(0, n, wait_sent, 0)


def per_device(n, transition, covariance):
    size = transition.shape[0]
    f32 = jnp.float32
    shape = jax.ShapeDtypeStruct(transition.shape, f32)
    return pl.pallas_call(
        functools.partial(kernel, n),
        out_shape=(shape, shape),
        in_specs=[pl.BlockSpec(memory_space=pl.ANY)] * 2,
        out_specs=(pl.BlockSpec(memory_space=pltpu.VMEM),) * 2,
        scratch_shapes=[
            pltpu.VMEM((n, size, size), f32),
            pltpu.VMEM((n, size, size), f32),
            pltpu.VMEM((n, size, size), f32),
            pltpu.VMEM((n, size, size), f32),
            pltpu.VMEM((n + 1, size, size), f32),
            pltpu.VMEM((size, size), jnp.bfloat16),
            pltpu.VMEM((size, size), jnp.bfloat16),
            pltpu.SemaphoreType.DMA((3,)),
            pltpu.SemaphoreType.DMA((2, 3)),
            pltpu.SemaphoreType.DMA((2, 3)),
            pltpu.SemaphoreType.DMA((2, n - 1, CHUNKS)),
            pltpu.SemaphoreType.DMA((2, n - 1, CHUNKS)),
            pltpu.SemaphoreType.DMA((n, CHUNKS)),
            pltpu.SemaphoreType.DMA((n + 1, CHUNKS)),
        ],
        compiler_params=pltpu.CompilerParams(
            collective_id=0, has_side_effects=True, vmem_limit_bytes=67043328
        ),
    )(transition, covariance)


def solution(mesh):
    n = mesh.shape["col"]
    assert mesh.shape["row"] == n == 4
    spec = P(("eq", "row"), "col")
    return jax.shard_map(
        functools.partial(per_device, n),
        mesh=mesh,
        in_specs=(spec, spec),
        out_specs=(spec, spec),
        check_vma=False,
    )
```

time: 606 us -> 290 us (0.48)
  waiting for transfers between devices: 367 us -> 0 us
  Pallas kernels: 0 us -> 282 us
  blocking collectives: 140 us -> 0 us
  matrix products: 82.5 us -> 0 us
  between operations: 13.8 us -> 0.65 us
    all_gather x5 -> x0, waiting for transfers between devices: 365 us -> none  [the longest x1 169 us: per_device(): product_row = lax.all_gather(product, 'col', axis=1, tiled=True)]
    pallas_call x0 -> x1, Pallas kernels: none -> 282 us  [per_device(): pl.pallas_call(functools.partial(kernel, n), out_shape=(shape, shape), in...]
    all_to_all x2 -> x0, blocking collectives: 140 us -> none  [the longest x1 88.7 us: per_device(): lax.all_to_all(lax.all_to_all(transition, 'row', split_axis=0, concat_axi...]
    dot_general x3 -> x0, matrix products: 82.5 us -> none  [the longest x2 54.8 us: add_one(): jnp.dot(matrix_row, pieces, precision=highest, preferred_element_type=jnp...]
  transfers between devices with their start and end apart: 5 -> 0, of which waited for: 4 -> 0; matrix products, arithmetic and copies ran while one was open for 9% -> 0% of each run, Pallas kernels for 0% -> 0%
where the time goes in v1:
time: 290 us; the launch traced here: 287 us
  Pallas kernels  282 us (97%)
  local copies, waits for them, and re-layouts  4.78 us (2%)
    pallas_call x1, Pallas kernels, per_device(): pl.pallas_call(functools.partial(kernel, n), out_shape=(shape, shape), in...  282 us

profile of v1, /device:TPU:0, one launch (start us, length us, event | category | flops | bytes accessed | tf_op | source)
XLA Modules:
  0.0 287.3 jit_solution(15775043577143661127)
XLA Ops:
  0.6 281.9 %shard_map.41 = (f32[768,768]{1,0:T(8,128)}, f32[768,768]{1,0:T(8,128)}) custom-call(f32[768,768]{1,0:T(8,128)} %a_ref.1, f32[768,768]{1,0:T(8,128)} %x_ref.1), custom_call_target="tpu_custom_call" | custom-call | tf_op jit(solution)/shard_map/pallas_call | solution.py:318
  282.5 0.0 copy-start
  282.5 3.4 %copy.6 = f32[768,768]{1,0:T(8,128)} copy(f32[768,768]{1,0:T(8,128)} %get-tuple-element.4) | data formatting | bytes 4718592
  285.9 0.0 copy-done
  285.9 1.4 copy.7
Async XLA Ops:
  282.5 3.4 %copy-start = (f32[768,768]{1,0:T(8,128)S(1)}, f32[768,768]{1,0:T(8,128)}, u32[]{:S(2)}) copy-start(f32[768,768]{1,0:T(8,128)} %get-tuple-element.5) | copy-start | bytes 7077892

commit v2 on v1

--- a/solution.py
+++ b/solution.py
@@ -172,6 +172,10 @@
             device_id_type=pl.DeviceIdType.MESH,
         ).wait_recv()
 
+    def far_first(i, low, high):
+        base = 0 if high - low == n else (block_of(low) // 2) * 2
+        return base + i, base + high - low - 1 - i
+
     def start_partials(c, low, high):
         per = size // TILE
 
@@ -185,42 +189,42 @@
 
         lax.fori_loop(low * per, high * per, tile, 0)
 
-        def send(m, carry):
-            d = block_of(m)
-
-            @pl.when((z == n - 1) & (d < z))
-            def _():
-                reduce_copy(LEFT, d, m, c).start()
-
-            @pl.when((z == 0) & (d > z))
-            def _():
-                reduce_copy(RIGHT, d, m, c).start()
-
-            return carry
-
-        lax.fori_loop(low, high, send, 0)
+        def send(i, carry):
+            to_left, to_right = far_first(i, low, high)
+
+            @pl.when((z == n - 1) & (to_left < z))
+            def _():
+                reduce_copy(LEFT, to_left, to_left, c).start()
+
+            @pl.when((z == 0) & (to_right > z))
+            def _():
+                reduce_copy(RIGHT, to_right, to_right, c).start()
+
+            return carry
+
+        lax.fori_loop(0, high - low, send, 0)
 
     def pass_on(hop, c, low, high):
-        def one(m, carry):
-            d = block_of(m)
-
-            def add():
+        def one(i, carry):
+            to_left, to_right = far_first(i, low, high)
+
+            def add(d):
                 reduce_wait(d, c)
                 partial[d, rows(c)] = partial[d, rows(c)] + arrived[d, rows(c)]
 
-            @pl.when((z == n - 1 - hop) & (d < z))
-            def _():
-                add()
-                reduce_copy(LEFT, d, m, c).start()
-
-            @pl.when((z == hop) & (d > z))
-            def _():
-                add()
-                reduce_copy(RIGHT, d, m, c).start()
-
-            return carry
-
-        lax.fori_loop(low, high, one, 0)
+            @pl.when((z == n - 1 - hop) & (to_left < z))
+            def _():
+                add(to_left)
+                reduce_copy(LEFT, to_left, to_left, c).start()
+
+            @pl.when((z == hop) & (to_right > z))
+            def _():
+                add(to_right)
+                reduce_copy(RIGHT, to_right, to_right, c).start()
+
+            return carry
+
+        lax.fori_loop(0, high - low, one, 0)
 
     def finish(c):
         update_ref[rows(c)] = x_col[r, rows(c)] + partial[z, rows(c)]
@@ -299,12 +303,10 @@
         for hop in range(n - 1):
             gather_each(hop, c, lambda copy: copy.wait_send())
 
-        def wait_sent(m, carry):
-            d = block_of(m)
-
+        def wait_sent(d, carry):
             @pl.when(d != z)
             def _():
-                reduce_copy(LEFT, d, m, c).wait_send()
+                reduce_copy(LEFT, d, d, c).wait_send()
 
             return carry
 

time: 290 us -> 277 us (0.955)
  Pallas kernels: 282 us -> 271 us
    pallas_call x1, Pallas kernels: 282 us -> 271 us  [per_device(): pl.pallas_call(functools.partial(kernel, n), out_shape=(shape, shape), in...]
where the time goes in v2:
time: 277 us
  Pallas kernels  271 us (98%)
  local copies, waits for them, and re-layouts  4.78 us (2%)
    pallas_call x1, Pallas kernels, per_device(): pl.pallas_call(functools.partial(kernel, n), out_shape=(shape, shape), in...  271 us

profile of v2, /device:TPU:0, one launch (start us, length us, event | category | flops | bytes accessed | tf_op | source)
XLA Modules:
  0.0 276.9 jit_solution(8062280996399473260)
XLA Ops:
  0.6 271.5 %shard_map.41 = (f32[768,768]{1,0:T(8,128)}, f32[768,768]{1,0:T(8,128)}) custom-call(f32[768,768]{1,0:T(8,128)} %a_ref.1, f32[768,768]{1,0:T(8,128)} %x_ref.1), custom_call_target="tpu_custom_call" | custom-call | tf_op jit(solution)/shard_map/pallas_call | solution.py:320
  272.1 0.0 copy-start
  272.1 3.4 %copy.6 = f32[768,768]{1,0:T(8,128)} copy(f32[768,768]{1,0:T(8,128)} %get-tuple-element.4) | data formatting | bytes 4718592
  275.5 0.0 copy-done
  275.5 1.4 copy.7
Async XLA Ops:
  272.1 3.4 %copy-start = (f32[768,768]{1,0:T(8,128)S(1)}, f32[768,768]{1,0:T(8,128)}, u32[]{:S(2)}) copy-start(f32[768,768]{1,0:T(8,128)} %get-tuple-element.5) | copy-start | bytes 7077892
